TPU v7x, 256 devices: a whole 4x4x8 slice. The times are simulated.
256 devices in a mesh: layer: 4 (over y), row: 8 (over x, z_lo), col: 8 (over z_hi, core).
Axes of the slice: x: 4, y: 4, z: 8 (z_hi: 4, z_lo: 2; z = z_hi * 2 + z_lo), core: 2. Of those that a mesh axis runs over, the one named last changes fastest.
Arguments:
- ancestor: float32 [8192, 8192], P('row', 'col'), may hold values from -768 to 3840, as said below
- coupling: bfloat16 [4, 8192, 1024], P('layer', ('row', 'col')), may hold values from -10 to 10
- fronts: float32 [4, 2, 512, 512], P('layer', None, None, ('row', 'col')), may hold values from -10 to 360, as said below
- tile_pattern: int32 [4, 2, 8], P('layer'), may hold values 0 or 1
Outputs:
- schur: float32 [8192, 8192], P('row', 'col')
- panel_factor: float32 [8192, 512], P(('row', 'col'))
- pivots: float32 [512], P(('row', 'col'))
Inputs may be any that keep to these rules, and one draw needn't show every extreme that they name: `ancestor`: symmetric and positive definite; the leading [512, 512] block of schur_0 stays positive definite after all layers' terms are subtracted. `fronts`: each [512, 512] block is symmetric and positive definite, with diagonal entries from 200 to 360 and other entries within -10 to 10.
All inputs are finite; a program needn't handle non-finite values. No bound on the sum of `tile_pattern` on one device may be relied on, other than what follows from the above.
Results may differ from a plain program's by a relative error of at most 0.0008.
Values may be sent and summed in bfloat16 or wider, within the bound.
A program may use at most 128 MiB of HBM per device.

v0:
```python
import jax
import jax.numpy as jnp
from jax import lax
from jax.sharding import PartitionSpec as P

S = 8192
TILE = 1024
P_SIZE = 512
NP = 2


def spread(value, axis, source):
    kept = jnp.where(lax.axis_index(axis) == source, value, 0).astype(value.dtype)
    return lax.psum(kept, axis)


def filled_up(lines, size):
    spare = -len(lines) % size
    return jnp.pad(lines, [(0, spare)] + [(0, 0)] * (lines.ndim - 1))


def spread_2(x, axis, root):
    lines = jnp.where(lax.axis_index(axis) == root, x, jnp.zeros_like(x)).reshape(
        -1, *x.shape[1:][-1:]
    )
    padded = filled_up(lines, lax.axis_size(axis))
    own = lax.psum_scatter(padded, axis, scatter_dimension=0, tiled=True)
    return lax.all_gather(own, axis, axis=0, tiled=True)[: len(lines)].reshape(x.shape)


def column_block(sender):
    row_count = lax.axis_size("row")
    col_count = lax.axis_size("col")
    col_place = lax.axis_index("col")
    first_root = col_place * row_count // col_count
    pieces = sender(first_root + 0)
    return pieces


def solve_rows(factor, columns):
    return lax.linalg.triangular_solve(
        factor, columns, left_side=False, lower=True, transpose_a=True
    )


def local(ancestor, coupling, fronts, tile_pattern):
    row_count = lax.axis_size("row")
    col_count = lax.axis_size("col")
    row_place = lax.axis_index("row")
    col_place = lax.axis_index("col")
    local_rows = S // (row_count * col_count)
    block_rows = S // row_count
    gathered = lax.all_gather(
        fronts.astype(jnp.bfloat16), ("row", "col"), axis=3, tiled=True
    ).astype(fronts.dtype)
    factors = jnp.linalg.cholesky(gathered[0])
    first_row = (row_place * col_count + col_place) * local_rows
    positions = first_row + lax.iota(jnp.int32, local_rows)
    onehot = (positions[:, None] // TILE == lax.iota(jnp.int32, S // TILE)[None, :]).astype(
        jnp.float32
    )
    row_masks = jnp.dot(onehot, tile_pattern[0].T.astype(jnp.float32))
    solved_parts = []
    for panel in range(NP):
        columns = (
            coupling[0, :, panel * P_SIZE : (panel + 1) * P_SIZE].astype(jnp.float32)
            * row_masks[:, panel : panel + 1]
        )
        solved_parts.append(solve_rows(factors[panel], columns))
    scaled = jnp.concatenate(solved_parts, 1).astype(jnp.bfloat16)
    row_side = lax.all_gather(scaled, "col", axis=0, tiled=True)
    col_side = column_block(lambda source: spread(row_side, "row", source))
    update = -lax.dot_general(
        row_side, col_side, (((1,), (1,)), ((), ())), preferred_element_type=jnp.float32
    )
    shared = lax.psum_scatter(
        update.astype(jnp.bfloat16), "layer", scatter_dimension=0, tiled=True
    ).astype(jnp.float32)
    summed = lax.all_gather(shared.astype(jnp.bfloat16), "layer", axis=0, tiled=True).astype(
        shared.dtype
    )
    leading = ancestor[:, :P_SIZE] + summed[:, :P_SIZE]
    global_rows = row_place * block_rows + lax.iota(jnp.int32, block_rows)
    trailing = None
    working = leading
    pivot_source = working[0:P_SIZE, 0:P_SIZE]
    pivot_block = spread(pivot_source, ("row", "col"), 0)
    pivot_chol = jnp.linalg.cholesky(pivot_block)
    keep_rows = (global_rows >= 0)[:, None]
    received = spread_2(working, "col", 0)
    solved = solve_rows(pivot_chol, received)
    panel_rows = jnp.where(keep_rows, solved, jnp.zeros_like(solved))
    panel_cols = column_block(lambda source: spread(panel_rows, "row", source))
    leading = leading - jnp.dot(
        panel_rows,
        panel_cols[:P_SIZE].T,
        precision=lax.Precision.HIGHEST,
        preferred_element_type=jnp.float32,
    )
    history = (panel_rows, panel_cols)
    panel_outs = lax.dynamic_slice_in_dim(panel_rows, col_place * local_rows, local_rows, 0)
    diagonal = jnp.diagonal(pivot_chol)
    pivot_outs = diagonal * diagonal
    trailing = ancestor[:, P_SIZE:] + summed[:, P_SIZE:]
    rows_part, cols_part = history
    trailing = trailing - jnp.dot(
        rows_part,
        cols_part[P_SIZE:].T,
        precision=lax.Precision.HIGHEST,
        preferred_element_type=jnp.float32,
    )
    schur = jnp.concatenate([leading, trailing], 1)
    pivot_share = pivot_outs.shape[0] // (row_count * col_count)
    flat_place = row_place * col_count + col_place
    my_pivots = lax.dynamic_slice_in_dim(pivot_outs, flat_place * pivot_share, pivot_share, 0)
    return (schur, panel_outs, my_pivots)


def solution(mesh):
    return jax.shard_map(
        local,
        mesh=mesh,
        in_specs=(
            P("row", "col"),
            P("layer", ("row", "col"), None),
            P("layer", None, None, ("row", "col")),
            P("layer", None, None),
        ),
        out_specs=(P("row", "col"), P(("row", "col"), None), P(("row", "col"))),
        check_vma=False,
    )
```

profile of v0, /device:TPU:1, one launch (start us, length us, event | category | flops | bytes accessed | tf_op | source)
XLA Modules:
  0.0 1092.7 jit_solution(2963737448343294521)
XLA Ops:
  12.0 115.7 %all-gather.5.cloned.1.call-done = bf16[1,2,512,512]{2,3,1,0:T(8,128)(2,1)} async-done(((bf16[1,2,512,8]{2,3,1,0:T(8,128)(2,1)}), bf16[1,2,512,512]{2,3,1,0:T(8,128)(2,1)}) %all-gather.5.cloned.1.call-update) | async-done | bytes 1048592 | tf_op jit(solution)/shard_map/all_gather | solution.py:53
  134.3 23.5 %custom-call.64 = f32[2,128,128]{2,1,0:T(8,128)S(1)} custom-call(f32[2,128,128]{2,1,0:T(8,128)S(1)} %cholesky.531), custom_call_target="Cholesky" | custom-call | tf_op jit(solution)/shard_map/jit(cholesky)/cholesky | solution.py:56
  157.8 19.7 %custom-call.65 = f32[2,1,128,128]{2,3,1,0:T(8,128)S(1)} custom-call(f32[2,1,128,128]{3,2,1,0:T(8,128)S(1)} %select_bitcast_fusion.2), custom_call_target="InvertDiagBlocksLowerTriangular" | custom-call | tf_op jit(solution)/shard_map/jit(cholesky)/cholesky | solution.py:56
  180.7 23.5 %custom-call.66 = f32[2,128,128]{2,1,0:T(8,128)S(1)} custom-call(f32[2,128,128]{2,1,0:T(8,128)S(1)} %cholesky.535), custom_call_target="Cholesky" | custom-call | tf_op jit(solution)/shard_map/jit(cholesky)/cholesky | solution.py:56
  204.2 19.8 %custom-call.67 = f32[2,1,128,128]{2,3,1,0:T(8,128)S(1)} custom-call(f32[2,1,128,128]{3,2,1,0:T(8,128)S(1)} %get-tuple-element.98), custom_call_target="InvertDiagBlocksLowerTriangular" | custom-call | tf_op jit(solution)/shard_map/jit(cholesky)/cholesky | solution.py:56
  226.1 23.5 %custom-call.68 = f32[2,128,128]{2,1,0:T(8,128)S(1)} custom-call(f32[2,128,128]{2,1,0:T(8,128)S(1)} %cholesky.540), custom_call_target="Cholesky" | custom-call | tf_op jit(solution)/shard_map/jit(cholesky)/cholesky | solution.py:56
  249.5 19.7 %custom-call.69 = f32[2,1,128,128]{2,3,1,0:T(8,128)S(1)} custom-call(f32[2,1,128,128]{3,2,1,0:T(8,128)S(1)} %get-tuple-element.96), custom_call_target="InvertDiagBlocksLowerTriangular" | custom-call | tf_op jit(solution)/shard_map/jit(cholesky)/cholesky | solution.py:56
  271.0 23.7 %custom-call.70 = f32[2,128,128]{2,1,0:T(8,128)S(1)} custom-call(f32[2,128,128]{2,1,0:T(8,128)S(1)} %convolution_subtract_fusion.7), custom_call_target="Cholesky" | custom-call | tf_op jit(solution)/shard_map/jit(cholesky)/cholesky | solution.py:56
  295.8 8.5 while.6
  304.2 39.3 %custom-call.78 = f32[4,128,128]{1,2,0:T(8,128)S(1)} custom-call(f32[4,128,128]{2,1,0:T(8,128)S(1)} %get-tuple-element.26), custom_call_target="InvertDiagBlocksLowerTriangular" | custom-call | tf_op jit(solution)/shard_map/triangular_solve/custom-call.14 | solution.py:41
  343.6 8.5 while.7
  352.1 39.7 %custom-call.79 = f32[4,128,128]{1,2,0:T(8,128)S(1)} custom-call(f32[4,128,128]{2,1,0:T(8,128)S(1)} %get-tuple-element.27), custom_call_target="InvertDiagBlocksLowerTriangular" | custom-call | tf_op jit(solution)/shard_map/triangular_solve/custom-call.14 | solution.py:41
  397.4 38.6 %all-gather.7.cloned.1.call-done = bf16[1024,1024]{0,1:T(8,128)(2,1)} async-done(((bf16[128,1024]{0,1:T(8,128)(2,1)}), bf16[1024,1024]{0,1:T(8,128)(2,1)}) %all-gather.7.cloned.1.call-update) | async-done | bytes 2097168 | tf_op jit(solution)/shard_map/all_gather | solution.py:71
  437.6 108.4 %all-reduce.6.cloned.1.call-done = bf16[1024,1024]{0,1:T(8,128)(2,1)} async-done(((bf16[1024,1024]{0,1:T(8,128)(2,1)}), bf16[1024,1024]{0,1:T(8,128)(2,1)}) %all-reduce.6.cloned.1.call-update) | async-done | bytes 2097168 | tf_op jit(solution)/shard_map/psum | solution.py:14
  546.0 5.3 negate_convert_fusion
  551.4 32.3 %reduce-scatter.3.cloned.1.call-done = bf16[256,1024]{0,1:T(8,128)(2,1)} async-done(((bf16[1024,1024]{0,1:T(8,128)(2,1)}), bf16[256,1024]{0,1:T(8,128)(2,1)}) %reduce-scatter.3.cloned.1.call-update) | async-done | bytes 524304 | tf_op jit(solution)/shard_map/reduce_scatter | solution.py:76
  590.4 29.9 %all-gather.9.cloned.1.call-done = bf16[1024,1024]{0,1:T(8,128)(2,1)} async-done(((bf16[256,1024]{0,1:T(8,128)(2,1)}), bf16[1024,1024]{0,1:T(8,128)(2,1)}) %all-gather.9.cloned.1.call-update) | async-done | bytes 2097168 | tf_op jit(solution)/shard_map/all_gather | solution.py:79
  628.4 186.2 %all-reduce.8.cloned.1.call-done = f32[512,512]{0,1:T(8,128)} async-done(((f32[512,512]{0,1:T(8,128)}), f32[512,512]{0,1:T(8,128)}) %all-reduce.8.cloned.1.call-update) | async-done | bytes 1048592 | tf_op jit(solution)/shard_map/psum | solution.py:14
  816.5 11.7 %cholesky.467 = f32[128,128]{1,0:T(8,128)S(1)} custom-call(f32[128,128]{1,0:T(8,128)S(1)} %cholesky.544), custom_call_target="Cholesky" | custom-call | tf_op jit(solution)/shard_map/jit(cholesky)/cholesky | solution.py:88
  828.4 9.8 custom-call.71
  839.0 11.7 %cholesky.483 = f32[128,128]{1,0:T(8,128)S(1)} custom-call(f32[128,128]{1,0:T(8,128)S(1)} %cholesky.548), custom_call_target="Cholesky" | custom-call | tf_op jit(solution)/shard_map/jit(cholesky)/cholesky | solution.py:88
  850.8 10.0 custom-call.72
  862.0 11.7 %cholesky.504 = f32[128,128]{1,0:T(8,128)S(1)} custom-call(f32[128,128]{1,0:T(8,128)S(1)} %cholesky.553), custom_call_target="Cholesky" | custom-call | tf_op jit(solution)/shard_map/jit(cholesky)/cholesky | solution.py:88
  873.9 9.8 custom-call.73
  884.5 11.7 %cholesky.521 = f32[128,128]{1,0:T(8,128)S(1)} custom-call(f32[128,128]{1,0:T(8,128)S(1)} %convolution_subtract_fusion.12), custom_call_target="Cholesky" | custom-call | tf_op jit(solution)/shard_map/jit(cholesky)/cholesky | solution.py:88
  901.8 8.6 while.5
  910.3 39.3 %custom-call.74 = f32[4,128,128]{1,2,0:T(8,128)S(1)} custom-call(f32[4,128,128]{2,1,0:T(8,128)S(1)} %get-tuple-element.19), custom_call_target="InvertDiagBlocksLowerTriangular" | custom-call | tf_op jit(solution)/shard_map/triangular_solve | solution.py:41
  961.9 4.7 gather_fusion
  968.1 99.3 %all-reduce.10.cloned.1.call-done = f32[1024,512]{0,1:T(8,128)} async-done(((f32[1024,512]{0,1:T(8,128)}), f32[1024,512]{0,1:T(8,128)}) %all-reduce.10.cloned.1.call-update) | async-done | bytes 2097168 | tf_op jit(solution)/shard_map/psum | solution.py:14
  1067.5 5.7 convolution_subtract_fusion
  1073.2 5.0 fusion
  1080.6 5.3 copy.74
  (191 shorter events, 90.0 us)
Async XLA Ops:
  7.2 120.6 %all-gather.5.cloned.1.call-start = ((), (), s32[]{:S(2)}) async-start(), calls=%async_computation.2 | async-start | bytes 1064960 | tf_op jit(solution)/shard_map/all_gather | solution.py:53
  8.6 427.5 %all-gather.7.cloned.1.call-start = ((), (), s32[]{:S(2)}) async-start(), calls=%async_computation.3 | async-start | bytes 2359296 | tf_op jit(solution)/shard_map/all_gather | solution.py:71
  130.6 2.0 copy-start.5
  132.9 1.3 copy-start.4
  295.7 96.1 %copy-start.10 = (f32[128,512]{1,0:T(8,128)S(1)}, f32[128,512]{1,0:T(8,128)}, u32[]{:S(2)}) copy-start(f32[128,512]{1,0:T(8,128)} %get-tuple-element.93) | copy-start | bytes 786436
  295.7 98.5 %copy-start.9 = (f32[128,512]{1,0:T(8,128)S(1)}, f32[128,512]{1,0:T(8,128)}, u32[]{:S(2)}) copy-start(f32[128,512]{1,0:T(8,128)} %get-tuple-element.94) | copy-start | bytes 786436
  397.4 148.6 %all-reduce.6.cloned.1.call-start = ((), (), s32[]{:S(2)}) async-start(), calls=%async_computation.4 | async-start | bytes 4194304 | tf_op jit(solution)/shard_map/psum | solution.py:14
  437.5 108.5 %copy-start.8 = (bf16[1024,1024]{0,1:T(8,128)(2,1)S(1)}, bf16[1024,1024]{0,1:T(8,128)(2,1)}, u32[]{:S(2)}) copy-start(bf16[1024,1024]{0,1:T(8,128)(2,1)} %all-gather.7.cloned.1.call-done) | copy-start | bytes 6291460
  437.5 146.1 %reduce-scatter.3.cloned.1.call-start = ((), (), s32[]{:S(2)}) async-start(), calls=%async_computation.5 | async-start | bytes 2621440 | tf_op jit(solution)/shard_map/reduce_scatter | solution.py:76
  551.3 69.0 %all-gather.9.cloned.1.call-start = ((), (), s32[]{:S(2)}) async-start(), calls=%async_computation.6 | async-start | bytes 2621440 | tf_op jit(solution)/shard_map/all_gather | solution.py:79
  583.7 230.9 %all-reduce.8.cloned.1.call-start = ((), (), s32[]{:S(2)}) async-start(), calls=%async_computation.9 | async-start | bytes 2097152 | tf_op jit(solution)/shard_map/psum | solution.py:14
  622.4 2.7 copy-start
  625.0 1.3 copy-start.2
  627.4 233.9 %reduce-scatter.5.cloned.1.call-start = ((), (), s32[]{:S(2)}) async-start(), calls=%async_computation.7 | async-start | bytes 2359296 | tf_op jit(solution)/shard_map/reduce_scatter | solution.py:27
  628.2 321.5 %all-gather.11.cloned.1.call-start = ((), (), s32[]{:S(2)}) async-start(), calls=%async_computation.8 | async-start | bytes 2359296 | tf_op jit(solution)/shard_map/all_gather | solution.py:28
  814.6 1.7 copy-start.6
  861.4 206.1 %all-reduce.10.cloned.1.call-start = ((), (), s32[]{:S(2)}) async-start(), calls=%async_computation.10 | async-start | bytes 4194304 | tf_op jit(solution)/shard_map/psum | solution.py:14
  949.7 4.1 copy-start.7
  1067.5 5.7 copy-start.1
  1067.5 5.7 copy-start.3
Sparse Core Ops, SparseCore 0:
  10.4 117.2 all-gather.4
  397.5 38.5 all-gather.6
  439.3 106.6 all-reduce.5
  551.5 32.1 reduce-scatter.2
  585.3 34.9 all-gather.8
  627.5 187.0 all-reduce.7
  817.2 42.0 reduce-scatter.4
  861.5 40.6 all-gather.10
  959.1 108.2 all-reduce.9
where the time goes:
time: 1100 us; the launch traced here: 1090 us
  waiting for transfers between devices  611 us (56%)
  other arithmetic  371 us (34%)
  local copies, waits for them, and re-layouts  53.8 us (5%)
  matrix products  37.8 us (3%)
  between operations  17.4 us (2%)
    psum x3, waiting for transfers between devices, spread(): return lax.psum(kept, axis)  394 us
    another operation x16, other arithmetic, local(): factors = jnp.linalg.cholesky(gathered[0])  154 us
    another operation x6, other arithmetic, solve_rows(): lax.linalg.triangular_solve(factor, columns, left_side=False, lower=True,...  119 us
    all_gather x1, waiting for transfers between devices, local(): lax.all_gather(fronts.astype(jnp.bfloat16), ('row', 'col'), axis=3, tiled...  116 us
    another operation x15, other arithmetic, local(): pivot_chol = jnp.linalg.cholesky(pivot_block)  79.2 us
    all_gather x1, waiting for transfers between devices, local(): row_side = lax.all_gather(scaled, 'col', axis=0, tiled=True)  38.6 us
    reduce_scatter x1, waiting for transfers between devices, local(): lax.psum_scatter(update.astype(jnp.bfloat16), 'layer', scatter_dimension=...  32.3 us
    all_gather x1, waiting for transfers between devices, local(): lax.all_gather(shared.astype(jnp.bfloat16), 'layer', axis=0, tiled=True)  29.9 us
  transfers between devices with their start and end apart: 9, of which 7 were waited for; matrix products, arithmetic and copies ran while one was open for 14% of the time, Pallas kernels for 0%

commit v1 on v0

--- a/solution.py
+++ b/solution.py
@@ -11,7 +11,7 @@
 
 def spread(value, axis, source):
     kept = jnp.where(lax.axis_index(axis) == source, value, 0).astype(value.dtype)
-    return lax.psum(kept, axis)
+    return jnp.sum(lax.all_gather(kept, axis), axis=0)
 
 
 def filled_up(lines, size):

time: 1100 us -> 1820 us (1.65)
  waiting for transfers between devices: 611 us -> 1280 us
  other arithmetic: 371 us -> 415 us
    all_gather x0 -> x3, waiting for transfers between devices: none -> 1010 us  [spread(): return jnp.sum(lax.all_gather(kept, axis), axis=0)]
    psum x3 -> x0, waiting for transfers between devices: 394 us -> none  [spread(): return lax.psum(kept, axis)]
    reduce_sum x0 -> x3, other arithmetic: none -> 42.4 us  [spread(): return jnp.sum(lax.all_gather(kept, axis), axis=0)]
    reduce_scatter x1, waiting for transfers between devices: 0.02 us -> 40.7 us  [spread_2(): own = lax.psum_scatter(padded, axis, scatter_dimension=0, tiled=True)]
    another operation x6 -> x7, other arithmetic: 119 us -> 119 us  [solve_rows(): lax.linalg.triangular_solve(factor, columns, left_side=False, lower=True,...]
  transfers between devices with their start and end apart: 9 -> 9, of which waited for: 7 -> 8; matrix products, arithmetic and copies ran while one was open for 14% -> 9% of each run, Pallas kernels for 0% -> 0%
where the time goes in v1:
time: 1820 us; the launch traced here: 1810 us
  waiting for transfers between devices  1280 us (70%)
  other arithmetic  415 us (23%)
  local copies, waits for them, and re-layouts  57.5 us (3%)
  matrix products  39.8 us (2%)
    all_gather x3, waiting for transfers between devices, spread(): return jnp.sum(lax.all_gather(kept, axis), axis=0)  1010 us
    another operation x16, other arithmetic, local(): factors = jnp.linalg.cholesky(gathered[0])  154 us
    another operation x7, other arithmetic, solve_rows(): lax.linalg.triangular_solve(factor, columns, left_side=False, lower=True,...  119 us
    all_gather x1, waiting for transfers between devices, local(): lax.all_gather(fronts.astype(jnp.bfloat16), ('row', 'col'), axis=3, tiled...  116 us
    another operation x15, other arithmetic, local(): pivot_chol = jnp.linalg.cholesky(pivot_block)  79.2 us
    reduce_sum x3, other arithmetic, spread(): return jnp.sum(lax.all_gather(kept, axis), axis=0)  42.4 us
    reduce_scatter x1, waiting for transfers between devices, spread_2(): own = lax.psum_scatter(padded, axis, scatter_dimension=0, tiled=True)  40.7 us
    all_gather x1, waiting for transfers between devices, local(): row_side = lax.all_gather(scaled, 'col', axis=0, tiled=True)  38.6 us
  transfers between devices with their start and end apart: 9, of which 8 were waited for; matrix products, arithmetic and copies ran while one was open for 9% of the time, Pallas kernels for 0%

profile of v1, /device:TPU:1, one launch (start us, length us, event | category | flops | bytes accessed | tf_op | source)
XLA Modules:
  0.0 1806.7 jit_solution(2040932722426375523)
XLA Ops:
  11.6 116.1 %all-gather.10.cloned.1.call-done = bf16[1,2,512,512]{2,3,1,0:T(8,128)(2,1)} async-done(((bf16[1,2,512,8]{2,3,1,0:T(8,128)(2,1)}), bf16[1,2,512,512]{2,3,1,0:T(8,128)(2,1)}) %all-gather.10.cloned.1.call-update) | async-done | bytes 1048592 | tf_op jit(solution)/shard_map/all_gather | solution.py:53
  134.3 23.5 %custom-call.64 = f32[2,128,128]{2,1,0:T(8,128)S(1)} custom-call(f32[2,128,128]{2,1,0:T(8,128)S(1)} %cholesky.531), custom_call_target="Cholesky" | custom-call | tf_op jit(solution)/shard_map/jit(cholesky)/cholesky | solution.py:56
  157.8 19.7 %custom-call.65 = f32[2,1,128,128]{2,3,1,0:T(8,128)S(1)} custom-call(f32[2,1,128,128]{3,2,1,0:T(8,128)S(1)} %select_bitcast_fusion.2), custom_call_target="InvertDiagBlocksLowerTriangular" | custom-call | tf_op jit(solution)/shard_map/jit(cholesky)/cholesky | solution.py:56
  180.7 23.5 %custom-call.66 = f32[2,128,128]{2,1,0:T(8,128)S(1)} custom-call(f32[2,128,128]{2,1,0:T(8,128)S(1)} %cholesky.535), custom_call_target="Cholesky" | custom-call | tf_op jit(solution)/shard_map/jit(cholesky)/cholesky | solution.py:56
  204.2 19.8 %custom-call.67 = f32[2,1,128,128]{2,3,1,0:T(8,128)S(1)} custom-call(f32[2,1,128,128]{3,2,1,0:T(8,128)S(1)} %get-tuple-element.73), custom_call_target="InvertDiagBlocksLowerTriangular" | custom-call | tf_op jit(solution)/shard_map/jit(cholesky)/cholesky | solution.py:56
  226.1 23.5 %custom-call.68 = f32[2,128,128]{2,1,0:T(8,128)S(1)} custom-call(f32[2,128,128]{2,1,0:T(8,128)S(1)} %cholesky.540), custom_call_target="Cholesky" | custom-call | tf_op jit(solution)/shard_map/jit(cholesky)/cholesky | solution.py:56
  249.5 19.7 %custom-call.69 = f32[2,1,128,128]{2,3,1,0:T(8,128)S(1)} custom-call(f32[2,1,128,128]{3,2,1,0:T(8,128)S(1)} %get-tuple-element.71), custom_call_target="InvertDiagBlocksLowerTriangular" | custom-call | tf_op jit(solution)/shard_map/jit(cholesky)/cholesky | solution.py:56
  271.0 23.7 %custom-call.70 = f32[2,128,128]{2,1,0:T(8,128)S(1)} custom-call(f32[2,128,128]{2,1,0:T(8,128)S(1)} %convolution_subtract_fusion.7), custom_call_target="Cholesky" | custom-call | tf_op jit(solution)/shard_map/jit(cholesky)/cholesky | solution.py:56
  295.8 8.5 while.6
  304.2 39.3 %custom-call.78 = f32[4,128,128]{1,2,0:T(8,128)S(1)} custom-call(f32[4,128,128]{2,1,0:T(8,128)S(1)} %get-tuple-element.26), custom_call_target="InvertDiagBlocksLowerTriangular" | custom-call | tf_op jit(solution)/shard_map/triangular_solve/custom-call.14 | solution.py:41
  346.0 8.0 while.7
  354.0 39.7 %custom-call.79 = f32[4,128,128]{1,2,0:T(8,128)S(1)} custom-call(f32[4,128,128]{2,1,0:T(8,128)S(1)} %get-tuple-element.27), custom_call_target="InvertDiagBlocksLowerTriangular" | custom-call | tf_op jit(solution)/shard_map/triangular_solve/custom-call.14 | solution.py:41
  397.0 38.6 %all-gather.12.cloned.1.call-done = bf16[1024,1024]{0,1:T(8,128)(2,1)} async-done(((bf16[128,1024]{0,1:T(8,128)(2,1)}), bf16[1024,1024]{0,1:T(8,128)(2,1)}) %all-gather.12.cloned.1.call-update) | async-done | bytes 2097168 | tf_op jit(solution)/shard_map/all_gather | solution.py:71
  437.1 326.6 %all-gather.20.cloned.1.call-done = bf16[8192,1024]{0,1:T(8,128)(2,1)} async-done(((bf16[1024,1024]{0,1:T(8,128)(2,1)}), bf16[8192,1024]{0,1:T(8,128)(2,1)}) %all-gather.20.cloned.1.call-update) | async-done | bytes 16777232 | tf_op jit(solution)/shard_map/all_gather | solution.py:14
  763.7 15.6 copy.75
  779.4 11.6 bitcast_reduce_fusion
  794.7 33.4 %reduce-scatter.3.cloned.1.call-done = bf16[256,1024]{1,0:T(8,128)(2,1)} async-done(((bf16[1024,1024]{1,0:T(8,128)(2,1)}), bf16[256,1024]{1,0:T(8,128)(2,1)}) %reduce-scatter.3.cloned.1.call-update) | async-done | bytes 524304 | tf_op jit(solution)/shard_map/reduce_scatter | solution.py:76
  828.2 34.6 %all-gather.14.cloned.1.call-done = bf16[1024,1024]{1,0:T(8,128)(2,1)} async-done(((bf16[256,1024]{1,0:T(8,128)(2,1)}), bf16[1024,1024]{1,0:T(8,128)(2,1)}) %all-gather.14.cloned.1.call-update) | async-done | bytes 2097168 | tf_op jit(solution)/shard_map/all_gather | solution.py:79
  870.0 40.7 %reduce-scatter.5.cloned.1.call-done = f32[128,512]{1,0:T(8,128)} async-done(((f32[1024,512]{1,0:T(8,128)}), f32[128,512]{1,0:T(8,128)}) %reduce-scatter.5.cloned.1.call-update) | async-done | bytes 262160 | tf_op jit(solution)/shard_map/reduce_scatter | solution.py:27
  910.8 367.9 %all-gather.22.cloned.1.call-done = f32[32768,512]{1,0:T(8,128)} async-done(((f32[512,512]{1,0:T(8,128)}), f32[32768,512]{1,0:T(8,128)}) %all-gather.22.cloned.1.call-update) | async-done | bytes 67108880 | tf_op jit(solution)/shard_map/all_gather | solution.py:14
  1278.7 21.4 %reduce_sum.31 = f32[512,512]{1,0:T(8,128)S(1)} reduce(f32[64,512,512]{2,1,0:T(8,128)} %bitcast.29, f32[]{:T(128)} %constant.333.clone.1), dimensions={0}, to_apply=%region_11.13 | reduce | flops 16515072 | bytes 68157440 | tf_op jit(solution)/shard_map/reduce_sum | solution.py:14
  1300.7 11.7 cholesky.467
  1312.5 9.8 custom-call.71
  1323.0 11.7 cholesky.483
  1334.8 10.0 custom-call.72
  1345.4 11.7 cholesky.504
  1357.2 9.8 custom-call.73
  1367.6 11.7 cholesky.521
  1385.2 8.2 while.5
  1393.4 39.3 %custom-call.74 = f32[4,128,128]{1,2,0:T(8,128)S(1)} custom-call(f32[4,128,128]{2,1,0:T(8,128)S(1)} %get-tuple-element.19), custom_call_target="InvertDiagBlocksLowerTriangular" | custom-call | tf_op jit(solution)/shard_map/triangular_solve | solution.py:41
  1459.3 317.9 %all-gather.18.cloned.1.call-done = f32[8,1024,512]{2,1,0:T(8,128)} async-done(((f32[1,1024,512]{2,1,0:T(8,128)}), f32[8,1024,512]{2,1,0:T(8,128)}) %all-gather.18.cloned.1.call-update) | async-done | bytes 16777232 | tf_op jit(solution)/shard_map/all_gather | solution.py:14
  1777.2 9.4 reduce_sum.32
  (182 shorter events, 107.1 us)
Async XLA Ops:
  7.2 120.6 %all-gather.10.cloned.1.call-start = ((), (), s32[]{:S(2)}) async-start(), calls=%async_computation.2 | async-start | bytes 1064960 | tf_op jit(solution)/shard_map/all_gather | solution.py:53
  8.6 427.0 %all-gather.12.cloned.1.call-start = ((), (), s32[]{:S(2)}) async-start(), calls=%async_computation.3 | async-start | bytes 2359296 | tf_op jit(solution)/shard_map/all_gather | solution.py:71
  130.6 2.0 copy-start.5
  132.9 1.3 copy-start.4
  295.4 48.1 %copy-start.12 = (f32[128,512]{1,0:T(8,128)S(1)}, f32[128,512]{1,0:T(8,128)}, u32[]{:S(2)}) copy-start(f32[128,512]{1,0:T(8,128)} %get-tuple-element.68) | copy-start | bytes 786436
  295.7 98.0 %copy-start.11 = (f32[128,512]{1,0:T(8,128)S(1)}, f32[128,512]{1,0:T(8,128)}, u32[]{:S(2)}) copy-start(f32[128,512]{1,0:T(8,128)} %get-tuple-element.69) | copy-start | bytes 786436
  396.9 366.8 %all-gather.20.cloned.1.call-start = ((), (), s32[]{:S(2)}) async-start(), calls=%async_computation.9 | async-start | bytes 18874368 | tf_op jit(solution)/shard_map/all_gather | solution.py:14
  437.1 391.1 %reduce-scatter.3.cloned.1.call-start = ((), (), s32[]{:S(2)}) async-start(), calls=%async_computation.4 | async-start | bytes 2621440 | tf_op jit(solution)/shard_map/reduce_scatter | solution.py:76
  779.4 11.6 copy-start.10
  794.7 68.1 %all-gather.14.cloned.1.call-start = ((), (), s32[]{:S(2)}) async-start(), calls=%async_computation.5 | async-start | bytes 2621440 | tf_op jit(solution)/shard_map/all_gather | solution.py:79
  828.2 82.6 %reduce-scatter.5.cloned.1.call-start = ((), (), s32[]{:S(2)}) async-start(), calls=%async_computation.6 | async-start | bytes 2359296 | tf_op jit(solution)/shard_map/reduce_scatter | solution.py:27
  862.8 2.8 copy-start.6
  865.6 2.6 copy-start
  868.3 1.7 copy-start.2
  868.3 410.4 %all-gather.22.cloned.1.call-start = ((), (), s32[]{:S(2)}) async-start(), calls=%async_computation.10 | async-start | bytes 68157440 | tf_op jit(solution)/shard_map/all_gather | solution.py:14
  870.0 562.8 %all-gather.16.cloned.1.call-start = ((), (), s32[]{:S(2)}) async-start(), calls=%async_computation.7 | async-start | bytes 2359296 | tf_op jit(solution)/shard_map/all_gather | solution.py:28
  910.8 866.4 %all-gather.18.cloned.1.call-start = ((), (), s32[]{:S(2)}) async-start(), calls=%async_computation.8 | async-start | bytes 18874368 | tf_op jit(solution)/shard_map/all_gather | solution.py:14
  1393.4 43.9 %copy-start.7 = (f32[512,512]{1,0:T(8,128)}, f32[512,512]{1,0:T(8,128)S(1)}, u32[]{:S(2)}) copy-start(f32[512,512]{1,0:T(8,128)S(1)} %get-tuple-element.248) | copy-start | bytes 3145732
  1432.8 4.5 copy-start.9
  1449.8 7.3 copy-start.8
  1786.6 5.6 copy-start.1
  1786.6 5.6 copy-start.3
Sparse Core Ops, SparseCore 0:
  10.4 117.2 all-gather.9
  397.0 38.5 all-gather.11
  438.0 325.7 all-gather.19
  794.8 33.2 reduce-scatter.2
  829.8 32.9 all-gather.13
  868.4 42.2 reduce-scatter.4
  912.6 366.0 all-gather.21
  1280.6 36.9 all-gather.15
  1448.8 328.3 all-gather.17
